TPU v7x, 32 devices: a whole 2x2x4 slice. The times are simulated.
32 devices in a mesh: pb: 2 (over core), row: 4 (over y, x), col: 4 (over z).
Axes of the slice: x: 2, y: 2, z: 4, core: 2. Of those that a mesh axis runs over, the one named last changes fastest.
Arguments:
- chol: bfloat16 [64, 1344, 1344], P('pb', 'row', 'col'), may hold values from -0.29882812 to 0.29882812
- amplitudes: bfloat16 [144, 1200], P(None, 'row'), may hold values from -0.59765625 to 0.59765625
Outputs:
- dressed: bfloat16 [64, 1344, 1344], P(('pb', 'row', 'col'))
- fock: float32 [1344, 1344], P('row', 'col')
All inputs are finite; a program needn't handle non-finite values.
Results may differ from a plain program's by a relative error of at most 0.02.
Values may be sent and summed in bfloat16 or wider, within the bound.
A program may use at most 128 MiB of HBM per device.

v0:
```python
import functools
import jax
import jax.numpy as jnp
from jax import lax
from jax.experimental import pallas as pl
from jax.experimental.pallas import tpu as pltpu
from jax.sharding import PartitionSpec as P

OG = 9
VG = 75
SH = 84
MESH = pl.DeviceIdType.MESH


def lanes(parts):
    return jnp.concatenate([p.astype(jnp.float32) for p in parts], axis=1).astype(jnp.bfloat16)


def pack(a, b, mid, low, rows):
    first, second = a.astype(jnp.float32), b.astype(jnp.float32)
    wide = jnp.concatenate([first[:, :mid], second[:, :mid]], axis=1).astype(jnp.bfloat16)
    thin = jnp.concatenate([first[:, mid:], second[:, mid:]], axis=0)
    pieces = [thin[k * rows : (k + 1) * rows] for k in range(thin.shape[0] // rows)]
    pieces.append(jnp.zeros((rows, 128 - low * len(pieces)), jnp.float32))
    return wide, jnp.concatenate(pieces, axis=1).astype(jnp.bfloat16)


def unpack(main, wide, thin, which, mid, low, rw):
    wide = wide.astype(jnp.float32)[:, which * mid : (which + 1) * mid]
    thin = thin.astype(jnp.float32)
    rows = thin.shape[0]
    pieces = [thin[:, k * low : (k + 1) * low] for k in range(2 * rw // rows)]
    thin = jnp.concatenate(pieces, axis=0)[which * rw : (which + 1) * rw]
    return jnp.concatenate([main.astype(jnp.float32), wide, thin], axis=1)


def dress(R, C, n, which, mid, low, mains, wides, thins, amps, pick, pick_t, primed, cols, put_dressed, put_fock):
    rw = mains.shape[1]
    th = rw * n
    for j in range(C):
        shift = None
        for i in range(C):
            pieces = []
            for m in range(n):
                s = (i * n + m) * C + j
                pieces.append(unpack(mains[s], wides[s], thins[s], which, mid, low, rw))
            tile = (pieces[0] if n == 1 else jnp.concatenate(pieces, axis=0)).astype(jnp.bfloat16)
            primed[i, j] = tile
            term = jnp.dot(amps[i], tile, preferred_element_type=jnp.float32)
            term = term.astype(jnp.bfloat16).astype(jnp.float32)
            shift = term if shift is None else shift + term
        hi = shift.astype(jnp.bfloat16)
        lo = (shift - hi.astype(jnp.float32)).astype(jnp.bfloat16)
        for i in range(C):
            placed = jnp.dot(pick[i], hi, preferred_element_type=jnp.float32)
            placed = placed + jnp.dot(pick[i], lo, preferred_element_type=jnp.float32)
            primed[i, j] = (primed[i, j].astype(jnp.float32) - placed).astype(jnp.bfloat16)
    weight = jnp.zeros((1, 1), jnp.float32)
    for i in range(C):
        occ = None
        for j in range(C):
            part = jnp.dot(primed[i, j], pick[j], preferred_element_type=jnp.float32)
            occ = part if occ is None else occ + part
        cols[i] = occ.astype(jnp.bfloat16)
        diag = occ * pick[i].astype(jnp.float32)
        weight = weight + jnp.sum(jnp.sum(diag, axis=1, keepdims=True), axis=0, keepdims=True)
    for i in range(C):
        strip = []
        for j in range(C):
            extra = jnp.dot(cols[i], amps[j], preferred_element_type=jnp.float32)
            tile = (primed[i, j].astype(jnp.float32) + extra).astype(jnp.bfloat16)
            primed[i, j] = tile
            strip.append(tile)
        put_dressed(i, lanes(strip))
    for j in range(C):
        rows = None
        for i in range(C):
            part = jnp.dot(pick_t[i], primed[i, j], preferred_element_type=jnp.float32)
            rows = part if rows is None else rows + part
        rows = rows.astype(jnp.bfloat16)
        for i in range(C):
            swapped = jnp.dot(cols[i], rows, preferred_element_type=jnp.float32)
            put_fock(i, j, 2.0 * weight * primed[i, j].astype(jnp.float32) - swapped)


def exchange_kernel(
    R, C, n, mid, low, rows, chol, amp, pick, pick_t,
    main_b, wide_all, thin_all, amps, dressed, fock,
    tails, wide_out, thin_out, own, amp_all, mains, wides, thins, primed, cols,
    send, recv, lsem,
):
    r = lax.axis_index("row")
    c = lax.axis_index("col")
    me = r * C + c
    rw = chol.shape[1]
    full = mains.shape[2]
    tail_in = pltpu.make_async_copy(chol.at[:, :, pl.ds(full, mid + low)], tails, lsem.at[0])
    tail_in.start()
    own_in = pltpu.make_async_copy(chol.at[pl.ds(me * 2, 2), :, pl.ds(0, full)], own, lsem.at[1])
    own_in.start()
    amp_in = pltpu.make_async_copy(amp, amp_all.at[r], lsem.at[2])
    amp_in.start()
    peers = [(dr, dc) for dr in range(R) for dc in range(C) if (dr, dc) != (0, 0)]
    peers.sort(key=lambda t: -min(t[1], C - t[1]))
    barrier = pltpu.get_barrier_semaphore()
    for dr, dc in peers:
        pl.semaphore_signal(
            barrier, inc=1, device_id={"row": lax.rem(r + dr, R), "col": lax.rem(c + dc, C)}, device_id_type=MESH
        )
    pl.semaphore_wait(barrier, len(peers))

    def move(kind, src, dst, dr, dc):
        return pltpu.make_async_remote_copy(
            src_ref=src,
            dst_ref=dst,
            send_sem=send.at[kind, dr * C + dc],
            recv_sem=recv.at[kind, dr * C + dc],
            device_id={"row": lax.rem(r + dr, R), "col": lax.rem(c + dc, C)},
            device_id_type=MESH,
        )

    amp_moves = [move(0, amp, amp_all.at[r], dr, 0) for dr in range(1, R)]
    for copy in amp_moves:
        copy.start()
    first, second = [], []
    for dr, dc in peers:
        to = lax.rem(r + dr, R) * C + lax.rem(c + dc, C)
        first.append(move(1, chol.at[to * 2, :, pl.ds(0, full)], mains.at[me], dr, dc))
        first[-1].start()
    tail_in.wait()

    def pack_one(d, carry):
        wide, thin = pack(tails[2 * d], tails[2 * d + 1], mid, low, rows)
        wide_out[d] = wide
        thin_out[d] = thin
        return carry

    lax.fori_loop(0, R * C, pack_one, 0)
    for dr, dc in peers:
        to = lax.rem(r + dr, R) * C + lax.rem(c + dc, C)
        first.append(move(2, wide_out.at[to], wide_all.at[me], dr, dc))
        first.append(move(3, thin_out.at[to], thin_all.at[me], dr, dc))
        first[-2].start()
        first[-1].start()
    for dr, dc in peers:
        to = lax.rem(r + dr, R) * C + lax.rem(c + dc, C)
        second.append(move(4, chol.at[to * 2 + 1, :, pl.ds(0, full)], main_b.at[me], dr, dc))
        second[-1].start()
    own_in.wait()
    amp_in.wait()
    mains[me] = own[0]
    local = [
        pltpu.make_async_copy(own.at[1], main_b.at[me], lsem.at[3]),
        pltpu.make_async_copy(wide_out.at[me], wide_all.at[me], lsem.at[4]),
        pltpu.make_async_copy(thin_out.at[me], thin_all.at[me], lsem.at[5]),
    ]
    for copy in local:
        copy.start()
    for copy in amp_moves:
        copy.wait()
    for i in range(C):
        amps[i] = amp_all[i] if n == 1 else lanes([amp_all[i * n + m] for m in range(n)])
    for copy in local:
        copy.wait()
    for copy in first:
        copy.wait()
    loads = [
        pltpu.make_async_copy(wide_all, wides, lsem.at[6]),
        pltpu.make_async_copy(thin_all, thins, lsem.at[7]),
    ]
    for copy in loads:
        copy.start()
    for copy in loads:
        copy.wait()
    th = rw * n

    def put_dressed(i, strip):
        dressed[0, pl.ds(i * th, th), :] = strip

    def put_fock(i, j, value):
        fock[i, j] = value

    dress(R, C, n, 0, mid, low, mains, wides, thins, amps, pick, pick_t, primed, cols, put_dressed, put_fock)
    for copy in second:
        copy.wait()


def dress_kernel(
    R, C, n, B, mid, low, mains, wides, thins, amps, pick, pick_t, before, before_fock,
    dressed, fock, primed, cols, held, result, partial, sem,
):
    share = C // B
    th = mains.shape[1] * n
    load = pltpu.make_async_copy(before, held, sem.at[0])
    load.start()
    load_fock = pltpu.make_async_copy(before_fock, partial, sem.at[1])
    load_fock.start()
    store = pltpu.make_async_copy(held, dressed.at[pl.ds(0, 1)], sem.at[2])
    final = pltpu.make_async_copy(result, dressed.at[pl.ds(1, 1)], sem.at[3])

    def put_dressed(i, strip):
        if i == 0:
            load.wait()
            store.start()
        result[0, pl.ds(i * th, th), :] = strip
        if i == C - 1:
            load_fock.wait()
            final.start()

    def put_fock(i, j, value):
        fock[j // share, i, j % share] = (partial[i, j] + value).astype(jnp.bfloat16)

    dress(R, C, n, 1, mid, low, mains, wides, thins, amps, pick, pick_t, primed, cols, put_dressed, put_fock)
    store.wait()
    final.wait()


def reduce_kernel(B, R, C, part, out, got1, half, got2, block, got3, s1, r1, s2, r2, s3, r3, s4, r4):
    b = lax.axis_index("pb")
    r = lax.axis_index("row")
    c = lax.axis_index("col")
    share = C // B
    barrier = pltpu.get_barrier_semaphore()
    for axis, index, size in (("pb", b, B), ("row", r, R), ("col", c, C)):
        for d in range(1, size):
            pl.semaphore_signal(barrier, inc=1, device_id={axis: lax.rem(index + d, size)}, device_id_type=MESH)
    pl.semaphore_wait(barrier, B + R + C - 3)
    order = list(range(1, R)) + [0]

    def to_half(k, d, e):
        to, row = lax.rem(b + e, B), lax.rem(r + d, R)
        return pltpu.make_async_remote_copy(
            src_ref=part.at[to, row, k], dst_ref=got1.at[e - 1, k, d],
            send_sem=s1.at[e, k, d], recv_sem=r1.at[e, k, d],
            device_id={"pb": to}, device_id_type=MESH,
        )

    def to_row(k, d):
        return pltpu.make_async_remote_copy(
            src_ref=half.at[k, d], dst_ref=got2.at[k, d], send_sem=s2.at[k, d], recv_sem=r2.at[k, d],
            device_id={"row": lax.rem(r + d, R)}, device_id_type=MESH,
        )

    def to_col(k, d):
        return pltpu.make_async_remote_copy(
            src_ref=block.at[k], dst_ref=got3.at[d - 1], send_sem=s3.at[k], recv_sem=r3.at[d],
            device_id={"col": b * share + k}, device_id_type=MESH,
        )

    for k in range(share):
        for d in order:
            for e in range(1, B):
                to_half(k, d, e).start()
    for k in range(share):
        for d in order:
            value = part[b, lax.rem(r + d, R), k].astype(jnp.float32)
            for e in range(1, B):
                to_half(k, d, e).wait()
                value = value + got1[e - 1, k, d].astype(jnp.float32)
            half[k, d] = value.astype(jnp.bfloat16)
            if d:
                to_row(k, d).start()
    for k in range(share):
        value = half[k, 0].astype(jnp.float32)
        for d in range(1, R):
            to_row(k, d).wait()
            value = value + got2[k, d].astype(jnp.float32)
        block[k] = value.astype(jnp.bfloat16)
        for d in range(1, C):
            @pl.when(lax.rem(c + d, C) == b * share + k)
            def _():
                to_col(k, d).start()

    for k in range(share):
        @pl.when(c == b * share + k)
        def _():
            total = block[k].astype(jnp.float32)
            for d in range(1, C):
                to_col(k, d).wait_recv()
                total = total + got3[d - 1].astype(jnp.float32)
            out[...] = total

    def to_pb(d):
        return pltpu.make_async_remote_copy(
            src_ref=out, dst_ref=out, send_sem=s4.at[d], recv_sem=r4.at[0],
            device_id={"pb": lax.rem(b + d, B)}, device_id_type=MESH,
        )

    mine = c // share == b

    @pl.when(mine)
    def _():
        for d in range(1, B):
            to_pb(d).start()
        for d in range(1, B):
            to_pb(d).wait_send()

    @pl.when(jnp.logical_not(mine))
    def _():
        to_pb(1).wait_recv()

    for k in range(share):
        @pl.when(c != b * share + k)
        def _():
            to_col(k, 1).wait_send()


def local(chol, amplitudes):
    B, R, C = lax.axis_size("pb"), lax.axis_size("row"), lax.axis_size("col")
    q_local, rw, cw = chol.shape
    n = cw // rw
    norb = C * cw
    occ = amplitudes.shape[0]
    groups = rw // SH
    full = cw // 128 * 128
    mid = 64
    low = cw - full - mid
    rows = 2 * rw // 7
    share = C // B
    amp = jnp.pad(amplitudes.reshape(occ, groups, VG), ((0, 0), (0, 0), (OG, 0))).reshape(occ, rw)
    orbital = lax.broadcasted_iota(jnp.int32, (C, cw, occ), 0) * cw + lax.broadcasted_iota(jnp.int32, (C, cw, occ), 1)
    index = lax.broadcasted_iota(jnp.int32, (C, cw, occ), 2)
    pick = (orbital == index // OG * SH + index % OG).astype(jnp.bfloat16)
    pick_t = jnp.transpose(pick, (0, 2, 1))
    hbm = pl.BlockSpec(memory_space=pl.ANY)
    vmem = pl.BlockSpec(memory_space=pltpu.VMEM)
    dma = pltpu.SemaphoreType.DMA
    bf16 = lambda *shape: pltpu.VMEM(shape, jnp.bfloat16)
    shape = lambda *dims: jax.ShapeDtypeStruct(dims, jnp.bfloat16)
    limit = 60 * 1024 * 1024
    N = R * C
    main_b, wide_all, thin_all, amps, before, before_fock = pl.pallas_call(
        functools.partial(exchange_kernel, R, C, n, mid, low, rows),
        out_shape=(
            shape(N, rw, full),
            shape(N, rw, 128),
            shape(N, rows, 128),
            shape(C, occ, cw),
            shape(1, norb, norb),
            jax.ShapeDtypeStruct((C, C, cw, cw), jnp.float32),
        ),
        in_specs=[hbm, hbm, vmem, vmem],
        out_specs=(hbm, hbm, hbm, vmem, vmem, vmem),
        scratch_shapes=[
            bf16(q_local, rw, mid + low),
            bf16(N, rw, 128),
            bf16(N, rows, 128),
            bf16(2, rw, full),
            bf16(R, occ, rw),
            bf16(N, rw, full),
            bf16(N, rw, 128),
            bf16(N, rows, 128),
            bf16(C, C, cw, cw),
            bf16(C, cw, occ),
            dma((5, N)),
            dma((5, N)),
            dma((8,)),
        ],
        compiler_params=pltpu.CompilerParams(collective_id=0, has_side_effects=True, vmem_limit_bytes=limit),
        name="exchange",
    )(chol, amp, pick, pick_t)
    dressed, fock = pl.pallas_call(
        functools.partial(dress_kernel, R, C, n, B, mid, low),
        out_shape=(shape(2, norb, norb), shape(B, C, share, cw, cw)),
        in_specs=[vmem] * 6 + [hbm, hbm],
        out_specs=(hbm, vmem),
        scratch_shapes=[
            bf16(C, C, cw, cw),
            bf16(C, cw, occ),
            bf16(1, norb, norb),
            bf16(1, norb, norb),
            pltpu.VMEM((C, C, cw, cw), jnp.float32),
            dma((4,)),
        ],
        compiler_params=pltpu.CompilerParams(vmem_limit_bytes=limit),
        name="dress",
    )(main_b, wide_all, thin_all, amps, pick, pick_t, before, before_fock)
    part = fock
    if n > 1:
        part = jnp.transpose(fock.reshape(B, C, share, n, rw, cw), (0, 1, 3, 2, 4, 5)).reshape(B, R, share, rw, cw)
    out = pl.pallas_call(
        functools.partial(reduce_kernel, B, R, C),
        out_shape=jax.ShapeDtypeStruct((rw, cw), jnp.float32),
        in_specs=[vmem],
        out_specs=vmem,
        scratch_shapes=[
            bf16(B - 1, share, R, rw, cw),
            bf16(share, R, rw, cw),
            bf16(share, R, rw, cw),
            bf16(share, rw, cw),
            bf16(C - 1, rw, cw),
            dma((B, share, R)), dma((B, share, R)), dma((share, R)), dma((share, R)),
            dma((share,)), dma((C,)), dma((B,)), dma((1,)),
        ],
        compiler_params=pltpu.CompilerParams(collective_id=1, has_side_effects=True, vmem_limit_bytes=limit),
        name="reduce",
    )(part)
    return dressed, out


def solution(mesh):
    return jax.shard_map(
        local,
        mesh=mesh,
        in_specs=(P("pb", "row", "col"), P(None, "row")),
        out_specs=(P(("pb", "row", "col"), None, None), P("row", "col")),
        check_vma=False,
    )
```

profile of v0, /device:TPU:9, one launch (start us, length us, event | category | flops | bytes accessed | tf_op | source)
XLA Modules:
  0.0 237.9 jit_solution(11123930894603433935)
XLA Ops:
  0.7 1.0 reshape.10
  1.7 0.2 pad.4
  1.9 0.8 reshape.11.amp
  2.7 1.0 fusion.1.pick_t
  3.6 1.1 fusion.pick
  4.7 171.3 %exchange.1 = (bf16[16,336,256]{2,1,0:T(8,128)(2,1)}, bf16[16,336,128]{2,1,0:T(8,128)(2,1)}, bf16[16,96,128]{2,1,0:T(8,128)(2,1)}, bf16[4,144,336]{2,1,0:T(8,128...) custom-call(bf16[32,336,336]{2,1,0:T(8,128)(2,1)} %chol.1, bf16[144,336]{1,0:T(8,128)(2,1)} %reshape.11.amp, ...), custom_call_target="tpu_custom_call" | custom-call | tf_op jit(solution)/shard_map/exchange/pallas_call | solution.py:332
  176.0 16.8 %dress.1 = (bf16[2,1344,1344]{2,1,0:T(8,128)(2,1)}, bf16[2,4,2,336,336]{4,3,2,1,0:T(8,128)(2,1)}) custom-call(bf16[16,336,256]{2,1,0:T(8,128)(2,1)} %get-tuple-element.10.mains, bf16[16,336,128]{2,1,0:T(8,128)(2,1)} %get-tuple-element.11.wides, bf16[16,96,128]{2,1,0:T(8,128)(2,1)} %get-tuple-element.12.thins, bf16[4,144,336]{2,1,0:T(8,128)(2,1)} %get-tuple-element.13.amps, ...), custom_call_target="tpu_custom_call" | custom-call | tf_op jit(solution)/shard_map/dress/pallas_call | solution.py:362
  192.8 43.2 %reduce.1 = f32[336,336]{1,0:T(8,128)} custom-call(bf16[2,4,2,336,336]{4,3,2,1,0:T(8,128)(2,1)} %get-tuple-element.17.part), custom_call_target="tpu_custom_call" | custom-call | tf_op jit(solution)/shard_map/reduce/pallas_call | solution.py:381
  236.1 1.9 copy.5
  (4 shorter events, 0.0 us)
where the time goes:
time: 239 us; the launch traced here: 238 us
  Pallas kernels  231 us (97%)
  local copies, waits for them, and re-layouts  3.84 us (2%)
    pallas_call x1, Pallas kernels, local(): pl.pallas_call(functools.partial(exchange_kernel, R, C, n, mid, low, rows...  171 us
    pallas_call x1, Pallas kernels, local(): pl.pallas_call(functools.partial(reduce_kernel, B, R, C), out_shape=jax.S...  43.2 us
    pallas_call x1, Pallas kernels, local(): pl.pallas_call(functools.partial(dress_kernel, R, C, n, B, mid, low), out...  16.8 us

commit v1 on v0

--- a/solution.py
+++ b/solution.py
@@ -1,5 +1,6 @@
 import functools
 import jax
+import numpy as np
 import jax.numpy as jnp
 from jax import lax
 from jax.experimental import pallas as pl
@@ -10,6 +11,13 @@
 VG = 75
 SH = 84
 MESH = pl.DeviceIdType.MESH
+
+
+def peer(index, mode, size):
+    if size & (size - 1):
+        return lax.rem(index + mode, size)
+    bits = [1 << k for k in range(size.bit_length() - 1)]
+    return sum(lax.rem(lax.rem(lax.div(index, bit), 2) + mode // bit % 2, 2) * bit for bit in bits)
 
 
 def lanes(parts):
@@ -25,16 +33,16 @@
     return wide, jnp.concatenate(pieces, axis=1).astype(jnp.bfloat16)
 
 
-def unpack(main, wide, thin, which, mid, low, rw):
+def unpack_tail(wide, thin, which, mid, low, rw):
     wide = wide.astype(jnp.float32)[:, which * mid : (which + 1) * mid]
     thin = thin.astype(jnp.float32)
     rows = thin.shape[0]
     pieces = [thin[:, k * low : (k + 1) * low] for k in range(2 * rw // rows)]
     thin = jnp.concatenate(pieces, axis=0)[which * rw : (which + 1) * rw]
-    return jnp.concatenate([main.astype(jnp.float32), wide, thin], axis=1)
-
-
-def dress(R, C, n, which, mid, low, mains, wides, thins, amps, pick, pick_t, primed, cols, put_dressed, put_fock):
+    return jnp.concatenate([wide, thin], axis=1)
+
+
+def dress(R, C, n, mains, tail, amps, pick, pick_t, primed, cols, put_dressed, put_fock):
     rw = mains.shape[1]
     th = rw * n
     for j in range(C):
@@ -43,8 +51,10 @@
             pieces = []
             for m in range(n):
                 s = (i * n + m) * C + j
-                pieces.append(unpack(mains[s], wides[s], thins[s], which, mid, low, rw))
-            tile = (pieces[0] if n == 1 else jnp.concatenate(pieces, axis=0)).astype(jnp.bfloat16)
+                pieces.append(jnp.concatenate([mains[s], tail[s]], axis=1))
+            tile = pieces[0]
+            if n > 1:
+                tile = jnp.concatenate([p.astype(jnp.float32) for p in pieces], axis=0).astype(jnp.bfloat16)
             primed[i, j] = tile
             term = jnp.dot(amps[i], tile, preferred_element_type=jnp.float32)
             term = term.astype(jnp.bfloat16).astype(jnp.float32)
@@ -84,9 +94,9 @@
 
 
 def exchange_kernel(
-    R, C, n, mid, low, rows, chol, amp, pick, pick_t,
-    main_b, wide_all, thin_all, amps, dressed, fock,
-    tails, wide_out, thin_out, own, amp_all, mains, wides, thins, primed, cols,
+    R, C, n, mid, low, rows, chol, amp, widen, pick, pick_t,
+    main_b, wide_all, thin_all, tail_b, amps, dressed, fock,
+    tails, wide_out, thin_out, own, amp_out, amp_all, mains, tail_a, wides, thins, primed, cols,
     send, recv, lsem,
 ):
     r = lax.axis_index("row")
@@ -98,15 +108,15 @@
     tail_in.start()
     own_in = pltpu.make_async_copy(chol.at[pl.ds(me * 2, 2), :, pl.ds(0, full)], own, lsem.at[1])
     own_in.start()
-    amp_in = pltpu.make_async_copy(amp, amp_all.at[r], lsem.at[2])
-    amp_in.start()
     peers = [(dr, dc) for dr in range(R) for dc in range(C) if (dr, dc) != (0, 0)]
-    peers.sort(key=lambda t: -min(t[1], C - t[1]))
+    peers.sort(key=lambda t: -t[1].bit_length())
     barrier = pltpu.get_barrier_semaphore()
     for dr, dc in peers:
         pl.semaphore_signal(
-            barrier, inc=1, device_id={"row": lax.rem(r + dr, R), "col": lax.rem(c + dc, C)}, device_id_type=MESH
-        )
+            barrier, inc=1, device_id={"row": peer(r, dr, R), "col": peer(c, dc, C)}, device_id_type=MESH
+        )
+    wide_amp = jnp.dot(amp[...], widen[...], preferred_element_type=jnp.float32).astype(jnp.bfloat16)
+    amp_out[...] = wide_amp
     pl.semaphore_wait(barrier, len(peers))
 
     def move(kind, src, dst, dr, dc):
@@ -115,18 +125,19 @@
             dst_ref=dst,
             send_sem=send.at[kind, dr * C + dc],
             recv_sem=recv.at[kind, dr * C + dc],
-            device_id={"row": lax.rem(r + dr, R), "col": lax.rem(c + dc, C)},
+            device_id={"row": peer(r, dr, R), "col": peer(c, dc, C)},
             device_id_type=MESH,
         )
 
-    amp_moves = [move(0, amp, amp_all.at[r], dr, 0) for dr in range(1, R)]
+    first, second = [], []
+    for dr, dc in peers:
+        to = peer(r, dr, R) * C + peer(c, dc, C)
+        first.append(move(1, chol.at[to * 2, :, pl.ds(0, full)], mains.at[me], dr, dc))
+        first[-1].start()
+    amp_moves = [move(0, amp_out, amp_all.at[r], dr, 0) for dr in range(1, R)]
     for copy in amp_moves:
         copy.start()
-    first, second = [], []
-    for dr, dc in peers:
-        to = lax.rem(r + dr, R) * C + lax.rem(c + dc, C)
-        first.append(move(1, chol.at[to * 2, :, pl.ds(0, full)], mains.at[me], dr, dc))
-        first[-1].start()
+    amp_all[r] = wide_amp
     tail_in.wait()
 
     def pack_one(d, carry):
@@ -137,17 +148,16 @@
 
     lax.fori_loop(0, R * C, pack_one, 0)
     for dr, dc in peers:
-        to = lax.rem(r + dr, R) * C + lax.rem(c + dc, C)
+        to = peer(r, dr, R) * C + peer(c, dc, C)
         first.append(move(2, wide_out.at[to], wide_all.at[me], dr, dc))
         first.append(move(3, thin_out.at[to], thin_all.at[me], dr, dc))
         first[-2].start()
         first[-1].start()
     for dr, dc in peers:
-        to = lax.rem(r + dr, R) * C + lax.rem(c + dc, C)
+        to = peer(r, dr, R) * C + peer(c, dc, C)
         second.append(move(4, chol.at[to * 2 + 1, :, pl.ds(0, full)], main_b.at[me], dr, dc))
         second[-1].start()
     own_in.wait()
-    amp_in.wait()
     mains[me] = own[0]
     local = [
         pltpu.make_async_copy(own.at[1], main_b.at[me], lsem.at[3]),
@@ -174,19 +184,26 @@
         copy.wait()
     th = rw * n
 
+    def open_tail(s, carry):
+        tail_a[s] = unpack_tail(wides[s], thins[s], 0, mid, low, rw).astype(jnp.bfloat16)
+        tail_b[s] = unpack_tail(wides[s], thins[s], 1, mid, low, rw).astype(jnp.bfloat16)
+        return carry
+
+    lax.fori_loop(0, R * C, open_tail, 0)
+
     def put_dressed(i, strip):
         dressed[0, pl.ds(i * th, th), :] = strip
 
     def put_fock(i, j, value):
         fock[i, j] = value
 
-    dress(R, C, n, 0, mid, low, mains, wides, thins, amps, pick, pick_t, primed, cols, put_dressed, put_fock)
+    dress(R, C, n, mains, tail_a, amps, pick, pick_t, primed, cols, put_dressed, put_fock)
     for copy in second:
         copy.wait()
 
 
 def dress_kernel(
-    R, C, n, B, mid, low, mains, wides, thins, amps, pick, pick_t, before, before_fock,
+    R, C, n, B, mains, tail, amps, pick, pick_t, before, before_fock,
     dressed, fock, primed, cols, held, result, partial, sem,
 ):
     share = C // B
@@ -210,7 +227,7 @@
     def put_fock(i, j, value):
         fock[j // share, i, j % share] = (partial[i, j] + value).astype(jnp.bfloat16)
 
-    dress(R, C, n, 1, mid, low, mains, wides, thins, amps, pick, pick_t, primed, cols, put_dressed, put_fock)
+    dress(R, C, n, mains, tail, amps, pick, pick_t, primed, cols, put_dressed, put_fock)
     store.wait()
     final.wait()
 
@@ -317,11 +334,14 @@
     low = cw - full - mid
     rows = 2 * rw // 7
     share = C // B
-    amp = jnp.pad(amplitudes.reshape(occ, groups, VG), ((0, 0), (0, 0), (OG, 0))).reshape(occ, rw)
-    orbital = lax.broadcasted_iota(jnp.int32, (C, cw, occ), 0) * cw + lax.broadcasted_iota(jnp.int32, (C, cw, occ), 1)
-    index = lax.broadcasted_iota(jnp.int32, (C, cw, occ), 2)
-    pick = (orbital == index // OG * SH + index % OG).astype(jnp.bfloat16)
-    pick_t = jnp.transpose(pick, (0, 2, 1))
+    virtual = np.arange(groups * VG)
+    widen = virtual[:, None] // VG * SH + OG + virtual[:, None] % VG == np.arange(rw)[None, :]
+    widen = jnp.asarray(widen, jnp.bfloat16)
+    index = np.arange(occ)
+    place = np.arange(norb)[:, None] == (index // OG * SH + index % OG)[None, :]
+    place = place.reshape(C, cw, occ)
+    pick = jnp.asarray(place, jnp.bfloat16)
+    pick_t = jnp.asarray(place.transpose(0, 2, 1), jnp.bfloat16)
     hbm = pl.BlockSpec(memory_space=pl.ANY)
     vmem = pl.BlockSpec(memory_space=pltpu.VMEM)
     dma = pltpu.SemaphoreType.DMA
@@ -329,25 +349,28 @@
     shape = lambda *dims: jax.ShapeDtypeStruct(dims, jnp.bfloat16)
     limit = 60 * 1024 * 1024
     N = R * C
-    main_b, wide_all, thin_all, amps, before, before_fock = pl.pallas_call(
+    main_b, wide_all, thin_all, tail_b, amps, before, before_fock = pl.pallas_call(
         functools.partial(exchange_kernel, R, C, n, mid, low, rows),
         out_shape=(
             shape(N, rw, full),
             shape(N, rw, 128),
             shape(N, rows, 128),
+            shape(N, rw, mid + low),
             shape(C, occ, cw),
             shape(1, norb, norb),
             jax.ShapeDtypeStruct((C, C, cw, cw), jnp.float32),
         ),
-        in_specs=[hbm, hbm, vmem, vmem],
-        out_specs=(hbm, hbm, hbm, vmem, vmem, vmem),
+        in_specs=[hbm, vmem, vmem, vmem, vmem],
+        out_specs=(hbm, hbm, hbm, vmem, vmem, vmem, vmem),
         scratch_shapes=[
             bf16(q_local, rw, mid + low),
             bf16(N, rw, 128),
             bf16(N, rows, 128),
             bf16(2, rw, full),
+            bf16(occ, rw),
             bf16(R, occ, rw),
             bf16(N, rw, full),
+            bf16(N, rw, mid + low),
             bf16(N, rw, 128),
             bf16(N, rows, 128),
             bf16(C, C, cw, cw),
@@ -358,11 +381,11 @@
         ],
         compiler_params=pltpu.CompilerParams(collective_id=0, has_side_effects=True, vmem_limit_bytes=limit),
         name="exchange",
-    )(chol, amp, pick, pick_t)
+    )(chol, amplitudes, widen, pick, pick_t)
     dressed, fock = pl.pallas_call(
-        functools.partial(dress_kernel, R, C, n, B, mid, low),
+        functools.partial(dress_kernel, R, C, n, B),
         out_shape=(shape(2, norb, norb), shape(B, C, share, cw, cw)),
-        in_specs=[vmem] * 6 + [hbm, hbm],
+        in_specs=[vmem] * 5 + [hbm, hbm],
         out_specs=(hbm, vmem),
         scratch_shapes=[
             bf16(C, C, cw, cw),
@@ -374,7 +397,7 @@
         ],
         compiler_params=pltpu.CompilerParams(vmem_limit_bytes=limit),
         name="dress",
-    )(main_b, wide_all, thin_all, amps, pick, pick_t, before, before_fock)
+    )(main_b, tail_b, amps, pick, pick_t, before, before_fock)
     part = fock
     if n > 1:
         part = jnp.transpose(fock.reshape(B, C, share, n, rw, cw), (0, 1, 3, 2, 4, 5)).reshape(B, R, share, rw, cw)

time: 239 us -> 235 us (0.983)
    pallas_call x1, Pallas kernels: 171 us -> 174 us  [local(): pl.pallas_call(functools.partial(exchange_kernel, R, C, n, mid, low, rows...]
    pallas_call x1, Pallas kernels: 43.2 us -> 40.4 us  [local(): pl.pallas_call(functools.partial(reduce_kernel, B, R, C), out_shape=jax.S...]
where the time goes in v1:
time: 235 us; the launch traced here: 234 us
  Pallas kernels  231 us (98%)
    pallas_call x1, Pallas kernels, local(): pl.pallas_call(functools.partial(exchange_kernel, R, C, n, mid, low, rows...  174 us
    pallas_call x1, Pallas kernels, local(): pl.pallas_call(functools.partial(reduce_kernel, B, R, C), out_shape=jax.S...  40.4 us
    pallas_call x1, Pallas kernels, local(): pl.pallas_call(functools.partial(dress_kernel, R, C, n, B), out_shape=(sh...  16.3 us

profile of v1, /device:TPU:9, one launch (start us, length us, event | category | flops | bytes accessed | tf_op | source)
XLA Modules:
  0.0 233.7 jit_solution(1936507426047686075)
XLA Ops:
  0.6 174.4 %exchange.1 = (bf16[16,336,256]{2,1,0:T(8,128)(2,1)}, bf16[16,336,128]{2,1,0:T(8,128)(2,1)}, bf16[16,96,128]{2,1,0:T(8,128)(2,1)}, bf16[16,336,80]{2,1,0:T(8,128...) custom-call(bf16[32,336,336]{2,1,0:T(8,128)(2,1)} %chol.1, ...), custom_call_target="tpu_custom_call" | custom-call | tf_op jit(solution)/shard_map/exchange/pallas_call | solution.py:352
  175.1 16.3 %dress.1 = (bf16[2,1344,1344]{2,1,0:T(8,128)(2,1)}, bf16[2,4,2,336,336]{4,3,2,1,0:T(8,128)(2,1)}) custom-call(bf16[16,336,256]{2,1,0:T(8,128)(2,1)} %get-tuple-element.9.mains, bf16[16,336,80]{2,1,0:T(8,128)(2,1)} %get-tuple-element.10.tail, bf16[4,144,336]{2,1,0:T(8,128)(2,1)} %get-tuple-element.11.amps, bf16[4,336,144]{2,1,0:T(8,128)(2,1)} %constant.7.clone.pick, ...), custom_call_target="tpu_custom_call" | custom-call | tf_op jit(solution)/shard_map/dress/pallas_call | solution.py:385
  191.4 40.4 %reduce.1 = f32[336,336]{1,0:T(8,128)} custom-call(bf16[2,4,2,336,336]{4,3,2,1,0:T(8,128)(2,1)} %get-tuple-element.15.part), custom_call_target="tpu_custom_call" | custom-call | tf_op jit(solution)/shard_map/reduce/pallas_call | solution.py:404
  231.9 1.9 copy.8
